TPU v7x, 32 devices: a whole 2x2x4 slice. The times are simulated.
32 devices in a mesh: section: 2 (over y), dp: 16 (over z, x, core).
Axes of the slice: x: 2, y: 2, z: 4, core: 2. Of those that a mesh axis runs over, the one named last changes fastest.
Arguments:
- student_head_logits: bfloat16 [32, 64, 32768], P('dp', None, 'section'), may hold values from -40 to 300
- hidden: bfloat16 [32, 64, 4096], P('dp', None, 'section'), may hold values from -6 to 6
- adapter_down: bfloat16 [4096, 32], P('section'), may hold values from -0.09375 to 0.09375
- adapter_up: bfloat16 [32, 32768], P(None, 'section'), may hold values from -1 to 1
- teacher_top_index: int32 [32, 64, 32], P('dp'), may hold values from 0 to 32767, as said below
- teacher_top_values: float32 [32, 64, 32], P('dp'), may hold values from -40 to 300
- teacher_other_logit: float32 [32, 64], P('dp'), may hold values from -40 to 300
- lengths: int32 [32], P('dp'), may hold values from 1 to 64, as said below
Outputs:
- distill_loss: float32 [], replicated
- grad_lora_a: float32 [4096, 32], P('section')
- grad_lora_b: float32 [32, 32768], P(None, 'section')
Inputs may be any that keep to these rules, and one draw needn't show every extreme that they name: `teacher_top_index`: the 32 ids of one position are distinct. `lengths`: the last sequence has all 64 positions sampled.
All inputs are finite; a program needn't handle non-finite values.
Results may differ from a plain program's by a relative error of at most 0.019.
Values may be sent and summed in bfloat16 or wider, within the bound.
A program may use at most 128 MiB of HBM per device.

v0:
```python
import jax
import jax.numpy as jnp
from jax import lax
from jax.sharding import PartitionSpec as P

SCALE_LOSS = 16384.0


def contract_rows(former, latter):
    return lax.dot_general(
        former, latter, (((0,), (0,)), ((), ())), preferred_element_type=jnp.float32
    )


def body(
    student_head_logits,
    hidden,
    adapter_down,
    adapter_up,
    teacher_top_index,
    teacher_top_values,
    teacher_other_logit,
    lengths,
):
    seq_total, seq_len, slice_width = student_head_logits.shape
    row_count = seq_total * seq_len
    output_logits = student_head_logits.reshape(row_count, slice_width)
    hidden_features = hidden.reshape(row_count, hidden.shape[2])
    token_ids = teacher_top_index.reshape(row_count, teacher_top_index.shape[2])
    values = teacher_top_values.reshape(row_count, teacher_top_values.shape[2])
    rest_logit = teacher_other_logit.reshape(row_count)
    reduced_partial = jnp.dot(hidden_features, adapter_down, preferred_element_type=jnp.float32)
    reduced_features = lax.psum(reduced_partial.astype(jnp.bfloat16), "section")
    logit_scores = output_logits.astype(jnp.float32) + jnp.dot(
        reduced_features, adapter_up, preferred_element_type=jnp.float32
    )
    offset = lax.axis_index("section") * slice_width
    local_ids = token_ids - offset
    owned_slot = (local_ids >= 0) & (local_ids < slice_width)
    safe_ids = jnp.where(owned_slot, local_ids, slice_width)
    row_ids = jnp.arange(row_count, dtype=jnp.int32)[:, None]
    support = (
        jnp.zeros((row_count, slice_width), jnp.float32).at[row_ids, safe_ids].set(1.0, mode="drop")
    )
    local_pick = jnp.take_along_axis(logit_scores, jnp.clip(local_ids, 0, slice_width - 1), axis=1)
    local_pick = jnp.where(owned_slot, local_pick, 0.0)
    local_top = jnp.max(logit_scores, axis=1)
    row_top = lax.pmax(local_top, "section")
    exp_scores = jnp.exp(logit_scores - row_top[:, None])
    row_total, tail_mass, picked = lax.psum(
        (jnp.sum(exp_scores, axis=1), jnp.sum(exp_scores * (1.0 - support), axis=1), local_pick),
        "section",
    )
    log_total = jnp.log(row_total)
    log_q = picked - row_top[:, None] - log_total[:, None]
    log_q_tail = jnp.log(tail_mass) - log_total
    teacher_top = jnp.maximum(jnp.max(values, axis=1), rest_logit)
    teacher_norm = (
        jnp.log(
            jnp.sum(jnp.exp(values - teacher_top[:, None]), axis=1)
            + jnp.exp(rest_logit - teacher_top)
        )
        + teacher_top
    )
    log_ratio = log_q - (values - teacher_norm[:, None])
    log_ratio_tail = log_q_tail - (rest_logit - teacher_norm)
    divergence = jnp.sum(jnp.exp(log_q) * log_ratio, axis=1) + jnp.exp(log_q_tail) * log_ratio_tail
    position = jnp.arange(seq_len, dtype=jnp.int32)
    valid_mask = (position[None, :] < lengths[:, None]).astype(jnp.float32).reshape(row_count)
    student_prob = exp_scores / row_total[:, None]
    log_gap = (
        jnp.broadcast_to(log_ratio_tail[:, None], (row_count, slice_width))
        .at[row_ids, safe_ids]
        .set(log_ratio, mode="drop")
    )
    score_gradient = (valid_mask[:, None] * student_prob * (log_gap - divergence[:, None])).astype(
        jnp.bfloat16
    )
    back_part = lax.dot_general(
        score_gradient, adapter_up, (((1,), (1,)), ((), ())), preferred_element_type=jnp.float32
    )
    reduced_gradient = lax.psum(back_part.astype(jnp.bfloat16), "section")
    grad_b = contract_rows(reduced_features, score_gradient)
    grad_a = contract_rows(hidden_features, reduced_gradient)
    loss_sum = jnp.sum(valid_mask * divergence)
    token_count = jnp.sum(lengths).astype(jnp.float32)
    grad_b, grad_a, loss_all, count_all = lax.psum((grad_b, grad_a, loss_sum, token_count), "dp")
    factor = SCALE_LOSS / count_all
    grad_b = grad_b * factor
    grad_a = grad_a * factor
    distill_loss = loss_all / count_all
    return (distill_loss, grad_a, grad_b)


def solution(mesh):
    return jax.shard_map(
        body,
        mesh=mesh,
        in_specs=(
            P("dp", None, "section"),
            P("dp", None, "section"),
            P("section", None),
            P(None, "section"),
            P("dp", None, None),
            P("dp", None, None),
            P("dp", None),
            P("dp"),
        ),
        out_specs=(P(), P("section", None), P(None, "section")),
        check_vma=False,
    )
```

profile of v0, /device:TPU:0, one launch (start us, length us, event | category | flops | bytes accessed | tf_op | source)
XLA Modules:
  0.0 362.9 jit_solution(11857839169983945676)
XLA Ops:
  7.2 0.8 broadcast_clamp_fusion
  8.1 0.8 reduce_max.21
  10.4 0.8 copy.23
  13.0 19.2 %scatter_custom_fusion = f32[2097152]{0:T(1024)} fusion(s32[4096]{0:T(1024)S(1)} %reshape.167, f32[4096]{0:T(1024)S(1)} %broadcast.174, f32[]{:T(128)} %constant.16.clone.1), kind=kCustom, calls=%fused_computation.9 | custom fusion | bytes 8388612
  32.2 5.7 %broadcast_subtract_fusion = f32[2097152]{0:T(1024)} fusion(f32[2097152]{0:T(1024)} %scatter_custom_fusion), kind=kLoop, calls=%fused_computation.8 | loop fusion | flops 2097152 | bytes 16777216 | tf_op jit(solution)/shard_map/sub | solution.py:51
  38.0 9.5 %reshape.160 = f32[128,16384]{1,0:T(8,128)} reshape(f32[2097152]{0:T(1024)} %broadcast_subtract_fusion) | data formatting | bytes 16777216 | tf_op jit(solution)/shard_map/sub | solution.py:51
  47.7 6.0 %psum.63 = bf16[128,32]{0,1:T(8,128)(2,1)S(1)} all-reduce(bf16[128,32]{0,1:T(8,128)(2,1)S(1)} %convolution_convert_fusion.1), channel_id=1, replica_groups=mesh['section'=2,'dp'=16] {'section'}, use_global_device_ids=true, to_apply=%region_0.0 | all-reduce | flops 4096 | bytes 16384 | tf_op jit(solution)/shard_map/psum | solution.py:33
  53.7 6.7 %fusion.6 = (f32[128]{0:T(128)S(1)}, f32[128,16384]{1,0:T(8,128)}) fusion(bf16[128,32]{0,1:T(8,128)(2,1)S(1)} %psum.63, bf16[32,16384]{1,0:T(8,128)(2,1)S(1)} %copy-done, bf16[128,16384]{1,0:T(8,128)(2,1)} %bitcast.29), kind=kOutput, calls=%fused_computation.41 | convolution fusion | flops 140509056 | bytes 13640192 | tf_op jit(solution)/shard_map/dot_general | solution.py:34
  60.4 4.9 %pmax.7 = f32[128]{0:T(128)S(1)} all-reduce(f32[128]{0:T(128)S(1)} %get-tuple-element.21), channel_id=1, replica_groups=mesh['section'=2,'dp'=16] {'section'}, use_global_device_ids=true, to_apply=%region_3.4 | all-reduce | flops 128 | bytes 1024 | tf_op jit(solution)/shard_map/pmax | solution.py:48
  65.5 110.9 %gather_fusion = f32[4096]{0:T(1024)S(1)} fusion(f32[128,16384]{1,0:T(8,128)} %get-tuple-element.22, s32[4096]{0:T(1024)S(1)} %reshape.161), kind=kCustom, calls=%fused_computation | custom fusion | bytes 65536 | tf_op jit(solution)/shard_map/jit(take_along_axis)/gather | solution.py:45
  176.7 6.9 %multiply_reduce_fusion = (f32[128]{0:T(128)S(1)}, f32[128]{0:T(128)S(1)}) fusion(f32[128,16384]{1,0:T(8,128)} %reshape.160, f32[128,16384]{1,0:T(8,128)} %get-tuple-element.22, f32[128]{0:T(128)S(1)} %pmax.7), kind=kLoop, calls=%fused_computation.5 | loop fusion | flops 8388352 | bytes 16778752 | tf_op jit(solution)/shard_map/reduce_sum | solution.py:51
  183.6 7.1 %all-reduce.2 = (f32[128,32]{0,1:T(8,128)S(1)}, f32[128]{0:T(128)S(1)}, f32[128]{0:T(128)S(1)}) all-reduce(f32[128,32]{0,1:T(8,128)S(1)} %select_select_fusion, f32[128]{0:T(128)S(1)} %get-tuple-element.4, f32[128]{0:T(128)S(1)} %get-tuple-element.3), channel_id=1, replica_groups=mesh['section'=2,'dp'=16] {'section'}, use_global_device_ids=true, to_apply=%region_1.2 | all-reduce | flops 4352 | bytes 34816 | tf_op jit(solution)/shard_map/psum | solution.py:50
  192.4 4.7 %copy.26 = f32[16,128,8,128]{3,1,2,0:T(8,128)} copy(f32[16,128,8,128]{3,2,1,0:T(8,128)S(1)} %broadcast_bitcast_fusion) | data formatting | bytes 16777216
  197.3 22.1 %scatter_fusion = f32[2097152]{0:T(1024)} fusion(f32[2097152]{0:T(1024)} %bitcast.28, s32[4096]{0:T(1024)S(1)} %reshape.167, f32[4096]{0:T(1024)S(1)} %reshape.175), kind=kCustom, calls=%fused_computation.2 | custom fusion | bytes 65536
  219.4 9.4 %reshape.157 = f32[128,16384]{1,0:T(8,128)} reshape(f32[2097152]{0:T(1024)} %scatter_fusion) | data formatting | bytes 16777216 | tf_op jit(solution)/shard_map/scatter | solution.py:74
  228.8 7.0 %multiply_convert_fusion = bf16[128,16384]{1,0:T(8,128)(2,1)S(1)} fusion(f32[128,16384]{1,0:T(8,128)} %reshape.157, f32[128,16384]{1,0:T(8,128)} %get-tuple-element.22, f32[128]{0:T(128)S(1)} %get-tuple-element.13, f32[128]{0:T(128)S(1)} %get-tuple-element.10, f32[128]{0:T(128)S(1)} %convert_element_type.30, f32[128]{0:T(128)S(1)} %pmax.7), kind=kLoop, calls=%fused_computation.4 | loop fusion | flops 12582912 | bytes 20973568 | tf_op jit(solution)/shard_map/convert_element_type | solution.py:76
  235.7 2.0 fusion.7
  237.7 1.5 convolution_convert_fusion
  239.2 5.0 %psum.69 = bf16[128,32]{0,1:T(8,128)(2,1)S(1)} all-reduce(bf16[128,32]{0,1:T(8,128)(2,1)S(1)} %convolution_convert_fusion), channel_id=1, replica_groups=mesh['section'=2,'dp'=16] {'section'}, use_global_device_ids=true, to_apply=%region_17.18 | all-reduce | flops 4096 | bytes 16384 | tf_op jit(solution)/shard_map/psum | solution.py:82
  244.2 0.9 convolution_bitcast_fusion
  246.4 36.1 %all-reduce = (f32[]{:T(128)}, f32[]{:T(128)}) all-reduce(f32[]{:T(128)} %get-tuple-element.12, f32[]{:T(128)S(6)} %convert_element_type.29), channel_id=1, replica_groups=mesh['section'=2,'dp'=16] {'dp'}, use_global_device_ids=true, to_apply=%region_13.14 | all-reduce | flops 2 | bytes 16 | tf_op jit(solution)/shard_map/psum | solution.py:87
  284.3 65.9 %all-reduce.5.cloned.1.call-done = (f32[2048,32]{0,1:T(8,128)}, f32[32,16384]{1,0:T(8,128)}) async-done(((f32[2048,32]{0,1:T(8,128)}, f32[32,16384]{1,0:T(8,128)}), (f32[2048,32]{0,1:T(8,128)}, f32[32,16384]{1,0:T(8,128)})) %all-reduce.5.cloned.1.call-update) | async-done | bytes 2359312 | tf_op jit(solution)/shard_map/psum | solution.py:87
  350.2 3.0 broadcast_multiply_fusion
  353.2 1.7 broadcast_multiply_fusion.1
  (50 shorter events, 6.7 us)
Async XLA Ops:
  7.2 46.5 %copy-start = (bf16[32,16384]{1,0:T(8,128)(2,1)S(1)}, bf16[32,16384]{1,0:T(8,128)(2,1)}, u32[]{:S(2)}) copy-start(bf16[32,16384]{1,0:T(8,128)(2,1)} %param.11) | copy-start | bytes 3145732
  7.2 343.0 %all-reduce.5.cloned.1.call-start = ((), (), s32[]{:S(2)}) async-start(), calls=%async_computation | async-start | bytes 4718592 | tf_op jit(solution)/shard_map/psum | solution.py:87
  38.0 9.5 %copy-start.1 = (bf16[2,64,2048]{2,1,0:T(8,128)(2,1)S(1)}, bf16[2,64,2048]{2,1,0:T(8,128)(2,1)}, u32[]{:S(2)}) copy-start(bf16[2,64,2048]{2,1,0:T(8,128)(2,1)} %param.9) | copy-start | bytes 1572868
  38.0 9.5 %copy-start.3 = (bf16[2048,32]{0,1:T(8,128)(2,1)S(1)}, bf16[2048,32]{0,1:T(8,128)(2,1)}, u32[]{:S(2)}) copy-start(bf16[2048,32]{0,1:T(8,128)(2,1)} %param.10) | copy-start | bytes 393220
  176.7 14.0 %copy-start.2 = (f32[2,64,32]{1,2,0:T(8,128)S(1)}, f32[2,64,32]{1,2,0:T(8,128)}, u32[]{:S(2)}) copy-start(f32[2,64,32]{1,2,0:T(8,128)} %param.13) | copy-start | bytes 49156
  176.7 14.3 %copy-start.4 = (s32[2]{0:T(128)S(1)}, s32[2]{0:T(128)}, u32[]{:S(2)}) copy-start(s32[2]{0:T(128)} %param.15) | copy-start | bytes 28
Sparse Core Ops, SparseCore 0:
  245.3 104.8 all-reduce.4
where the time goes:
time: 367 us; the launch traced here: 363 us
  local copies, waits for them, and re-layouts  179 us (49%)
  waiting for transfers between devices  65.9 us (18%)
  blocking collectives  59.1 us (16%)
  other arithmetic  29.5 us (8%)
  between operations  17.7 us (5%)
  matrix products  11.4 us (3%)
    gather x5, local copies, waits for them, and re-layouts, body(): jnp.take_along_axis(logit_scores, jnp.clip(local_ids, 0, slice_width - 1)...  111 us
    psum x1, waiting for transfers between devices, body(): lax.psum((grad_b, grad_a, loss_sum, token_count), 'dp')  65.9 us
    unnamed x18, local copies, waits for them, and re-layouts  47.6 us
    psum x1, blocking collectives, body(): lax.psum((grad_b, grad_a, loss_sum, token_count), 'dp')  36.1 us
    sub x1, local copies, waits for them, and re-layouts, body(): 1.0 - support  9.46 us
    scatter x1, local copies, waits for them, and re-layouts, body(): log_gap = jnp.broadcast_to(log_ratio_tail[:, None], (row_count, slice_wid...  9.39 us
  transfers between devices with their start and end apart: 1, of which 1 were waited for; matrix products, arithmetic and copies ran while one was open for 0% of the time, Pallas kernels for 0%

commit v1 on v0

v1 whole, which is shorter than its diff:
```python
import functools

import jax
import jax.numpy as jnp
from jax import lax
from jax.experimental import pallas as pl
from jax.experimental.pallas import tpu as pltpu
from jax.sharding import PartitionSpec as P

SCALE_LOSS = 16384.0
LANES = 128
F32 = jnp.float32
BF16 = jnp.bfloat16
MESH = pl.DeviceIdType.MESH


def remote(src, dst, send, recv, axis, target):
    return pltpu.make_async_remote_copy(
        src_ref=src,
        dst_ref=dst,
        send_sem=send,
        recv_sem=recv,
        device_id={axis: target},
        device_id_type=MESH,
    )


class SectionExchange:
    def __init__(self, buf, send, recv, n):
        self.buf = buf
        me = lax.axis_index("section")
        self.copies = [
            remote(buf.at[me], buf.at[me], send.at[j - 1], recv.at[j - 1], "section", lax.rem(me + j, n))
            for j in range(1, n)
        ]

    def start(self):
        for c in self.copies:
            c.start()

    def wait(self):
        for c in self.copies:
            c.wait()


class DataReduce:
    def __init__(self, part, pair, slots, total, sems, n):
        self.part, self.pair, self.slots, self.total = part, pair, slots, total
        self.sems = sems
        self.n2 = n // 2
        self.width = part.shape[1] // n
        self.half = part.shape[1] // 2
        me = lax.axis_index("dp")
        self.core = lax.rem(me, 2)
        self.chip = me // 2
        self.mate = me + 1 - 2 * self.core

    def peer(self, j):
        return lax.rem(self.chip + j, self.n2) * 2 + self.core

    def cols(self, half, piece):
        start = pl.multiple_of(half * self.half + piece * self.width, LANES)
        return pl.ds(start, self.width)

    def order(self):
        return list(range(1, self.n2)) + [0]

    def start_pair(self):
        self.pair_copies = {}
        for j in self.order():
            piece = lax.rem(self.chip + j, self.n2)
            c = remote(
                self.part.at[:, self.cols(1 - self.core, piece)],
                self.pair.at[:, self.cols(0, piece)],
                self.sems.at[0, j],
                self.sems.at[1, j],
                "dp",
                self.mate,
            )
            c.start()
            self.pair_copies[j] = c

    def start_scatter(self):
        self.scatter_copies = {}
        for j in self.order():
            piece = lax.rem(self.chip + j, self.n2)
            self.pair_copies[j].wait()
            mine = self.cols(self.core, piece)
            both = self.part[:, mine].astype(F32) + self.pair[:, self.cols(0, piece)].astype(F32)
            self.part[:, mine] = both.astype(BF16)
            if j:
                c = remote(
                    self.part.at[:, mine],
                    self.slots.at[j - 1],
                    self.sems.at[2, j],
                    self.sems.at[3, j],
                    "dp",
                    self.peer(j),
                )
                c.start()
                self.scatter_copies[j] = c

    def start_gather(self):
        mine = self.cols(self.core, self.chip)
        acc = self.part[:, mine].astype(F32)
        for j in range(1, self.n2):
            self.scatter_copies[j].wait()
            acc = acc + self.slots[j - 1].astype(F32)
        self.total[:, mine] = acc.astype(BF16)
        self.gather_copies = {}
        for j in self.order():
            c = remote(
                self.total.at[:, mine],
                self.total.at[:, mine],
                self.sems.at[4, j],
                self.sems.at[5, j],
                "dp",
                self.peer(j) if j else self.mate,
            )
            c.start()
            self.gather_copies[j] = c

    def forward(self):
        forwards = []
        for j in range(1, self.n2):
            piece = lax.rem(self.chip + self.n2 - j, self.n2)
            theirs = self.cols(self.core, piece)
            self.gather_copies[j].wait()
            c = remote(
                self.total.at[:, theirs],
                self.total.at[:, theirs],
                self.sems.at[6, j],
                self.sems.at[7, j],
                "dp",
                self.mate,
            )
            c.start()
            forwards.append(c)
        self.gather_copies[0].wait()
        for c in forwards:
            c.wait()


def contract(former, latter, dims):
    return lax.dot_general(former, latter, (dims, ((), ())), preferred_element_type=F32)


def kernel(
    n_sec,
    n_dp,
    seq_len,
    lengths_ref,
    logits_ref,
    hidden_ref,
    down_ref,
    up_ref,
    ids_ref,
    values_ref,
    other_ref,
    loss_ref,
    grad_a_ref,
    grad_b_ref,
    scores_ref,
    teach_ref,
    grad_ref,
    hi_ref,
    lo_ref,
    piece_ref,
    low_buf,
    stat_buf,
    back_buf,
    acc_ref,
    row_ref,
    b_part,
    b_pair,
    b_slots,
    b_total,
    a_part,
    a_pair,
    a_slots,
    a_total,
    loss_part,
    loss_slots,
    sec_send,
    sec_recv,
    b_sems,
    a_sems,
    loss_sems,
):
    rows, width = logits_ref.shape
    features = hidden_ref.shape[1]
    topk = ids_ref.shape[1]
    rank = up_ref.shape[0]
    blocks = width // LANES
    sec = lax.axis_index("section")
    me = lax.axis_index("dp")
    n2 = n_dp // 2
    core = lax.rem(me, 2)
    chip = me // 2
    mate = me + 1 - 2 * core

    barrier = pltpu.get_barrier_semaphore()
    for j in range(1, n_sec):
        pl.semaphore_signal(barrier, inc=1, device_id={"section": lax.rem(sec + j, n_sec)}, device_id_type=MESH)
    pl.semaphore_signal(barrier, inc=1, device_id={"dp": mate}, device_id_type=MESH)
    for j in range(1, n2):
        pl.semaphore_signal(
            barrier, inc=1, device_id={"dp": lax.rem(chip + j, n2) * 2 + core}, device_id_type=MESH
        )

    low_part = jnp.dot(hidden_ref[...], down_ref[...], preferred_element_type=F32)
    low_buf[sec] = low_part.astype(BF16)
    pl.semaphore_wait(barrier, n_sec - 1 + 1 + n2 - 1)
    low_swap = SectionExchange(low_buf, sec_send.at[0], sec_recv.at[0], n_sec)
    low_swap.start()

    values = values_ref[...]
    seq_total = rows // seq_len
    eye = lax.broadcasted_iota(jnp.int32, (seq_len, seq_len), 0) == lax.broadcasted_iota(
        jnp.int32, (seq_len, seq_len), 1
    )
    rest = jnp.concatenate(
        [
            jnp.sum(jnp.where(eye, jnp.broadcast_to(other_ref[s : s + 1, :], (seq_len, seq_len)), 0.0), axis=1, keepdims=True)
            for s in range(seq_total)
        ],
        axis=0,
    )
    teacher_top = jnp.maximum(jnp.max(values, axis=1, keepdims=True), rest)
    teacher_norm = (
        jnp.log(jnp.sum(jnp.exp(values - teacher_top), axis=1, keepdims=True) + jnp.exp(rest - teacher_top))
        + teacher_top
    )
    log_t_tail = rest - teacher_norm
    shifted = jnp.minimum(values - teacher_norm, 0.0) - 1.0
    first = shifted.astype(BF16).astype(F32)
    second = (shifted - first).astype(BF16).astype(F32)
    third = shifted - first - second
    ids = ids_ref[...]
    high = ((ids >> 7) - sec * blocks).astype(F32)
    low = (ids & (LANES - 1)).astype(F32)
    hi_ref[...] = jnp.full((rows, LANES), -1.0, F32)
    lo_ref[...] = jnp.full((rows, LANES), -1.0, F32)
    piece_ref[...] = jnp.zeros((rows, LANES), F32)
    for i, piece in enumerate((first, second, third)):
        span = slice(i * topk, (i + 1) * topk)
        hi_ref[:, span] = high
        lo_ref[:, span] = low
        piece_ref[:, span] = piece
    block_iota = lax.broadcasted_iota(jnp.int32, (blocks, LANES), 0).astype(F32)
    lane_iota = lax.broadcasted_iota(jnp.int32, (LANES, LANES), 0).astype(F32)

    def place_row(r):
        left = jnp.where(block_iota == hi_ref[pl.ds(r, 1), :], piece_ref[pl.ds(r, 1), :], 0.0)
        right = jnp.where(lane_iota == lo_ref[pl.ds(r, 1), :], 1.0, 0.0)
        teach_ref[pl.ds(r, blocks, stride=rows), :] = contract(
            left.astype(BF16), right.astype(BF16), ((1,), (1,))
        )

    unroll = 4

    @pl.loop(0, rows // unroll)
    def _(step):
        for u in range(unroll):
            place_row(step * unroll + u)

    low_swap.wait()
    low_sum = low_buf[0].astype(F32)
    for s in range(1, n_sec):
        low_sum = low_sum + low_buf[s].astype(F32)
    low_rank = low_sum.astype(BF16)
    low_rank_t = low_sum.T.astype(BF16)

    span = 256

    def score_step(step, top):
        cols = pl.ds(pl.multiple_of(step * span, span), span)
        block = logits_ref[:, cols].astype(F32) + jnp.dot(
            low_rank, up_ref[:, cols], preferred_element_type=F32
        )
        scores_ref[:, cols] = block
        for i in range(span // LANES):
            top = jnp.maximum(top, block[:, i * LANES : (i + 1) * LANES])
        return top

    top = lax.fori_loop(
        0, width // span, score_step, jnp.full((rows, LANES), -3.0e38, F32), unroll=2
    )
    local_top = jnp.max(top, axis=1, keepdims=True)
    row_ref[0] = jnp.broadcast_to(local_top, (rows, LANES))

    group = 32
    lane = lax.broadcasted_iota(jnp.int32, (group, LANES), 1)
    chunk = 4

    @pl.loop(0, rows // group)
    def _(g):
        base = pl.multiple_of(g * group, group)
        here = pl.ds(base, group)
        peak = row_ref[0, here, :]

        def step_sum(step, carry):
            total, tail, mass, cross = carry
            for i in range(chunk):
                b = step * chunk + i
                s = scores_ref[here, pl.ds(pl.multiple_of(b * LANES, LANES), LANES)]
                t = teach_ref[pl.ds(pl.multiple_of(b * rows + base, group), group), :]
                gap = s - peak
                e = jnp.exp(gap)
                named = t < 0.0
                e_named = jnp.where(named, e, 0.0)
                total = total + e
                tail = tail + jnp.where(named, 0.0, e)
                mass = mass + e_named
                cross = cross + e_named * (gap - t)
            return total, tail, mass, cross

        zero = jnp.zeros((group, LANES), F32)
        sums = lax.fori_loop(0, blocks // chunk, step_sum, (zero, zero, zero, zero))
        packed = peak
        for i, x in enumerate(sums):
            packed = jnp.where(lane == i + 1, jnp.sum(x, axis=1, keepdims=True), packed)
        stat_buf[sec, here, :] = packed

    stat_swap = SectionExchange(stat_buf, sec_send.at[1], sec_recv.at[1], n_sec)
    stat_swap.start()
    position = lax.broadcasted_iota(jnp.int32, (seq_len, 1), 0)
    valid = jnp.concatenate(
        [(position < lengths_ref[s]).astype(F32) for s in range(seq_total)], axis=0
    )
    count = lengths_ref[0]
    for s in range(1, seq_total):
        count = count + lengths_ref[s]
    stat_swap.wait()

    tops = [stat_buf[s, :, 0:1] for s in range(n_sec)]
    row_top = functools.reduce(jnp.maximum, tops)
    shrink = [jnp.exp(t - row_top) for t in tops]
    row_total = sum(stat_buf[s, :, 1:2] * shrink[s] for s in range(n_sec))
    tail_mass = sum(stat_buf[s, :, 2:3] * shrink[s] for s in range(n_sec))
    log_total = jnp.log(row_total)
    log_tail = jnp.log(tail_mass) - log_total
    tail_ratio = log_tail - log_t_tail
    divergence = jnp.exp(log_tail) * tail_ratio
    for s in range(n_sec):
        shift = tops[s] - row_top - log_total - 1.0
        divergence = divergence + (shrink[s] / row_total) * (
            stat_buf[s, :, 4:5] + stat_buf[s, :, 3:4] * shift
        )
    own_shift = local_top - row_top - log_total - 1.0
    full = (rows, LANES)
    row_ref[1] = jnp.broadcast_to(valid * jnp.exp(local_top - row_top) / row_total, full)
    row_ref[2] = jnp.broadcast_to(own_shift - divergence, full)
    row_ref[3] = jnp.broadcast_to(tail_ratio - divergence, full)

    loss_sum = jnp.sum(valid * divergence, axis=0, keepdims=True)
    tile_lane = lax.broadcasted_iota(jnp.int32, (8, LANES), 1)
    loss_part[0] = jnp.where(tile_lane == 0, loss_sum, jnp.where(tile_lane == 1, count.astype(F32), 0.0))
    loss_pair = remote(loss_part.at[0], loss_part.at[1], loss_sems.at[0, 0], loss_sems.at[1, 0], "dp", mate)
    loss_pair.start()

    acc_ref[...] = jnp.zeros_like(acc_ref)
    if b_part.shape[1] > width:
        b_part[:, width:] = jnp.zeros((rank, b_part.shape[1] - width), BF16)
    if a_part.shape[1] > features:
        a_part[:, features:] = jnp.zeros((rank, a_part.shape[1] - features), BF16)
    wide = 512

    @pl.loop(0, width // wide)
    def _(step):
        for g in range(rows // group):
            here = pl.ds(g * group, group)
            peak, scale = row_ref[0, here, :], row_ref[1, here, :]
            named_add, tail_add = row_ref[2, here, :], row_ref[3, here, :]
            for i in range(wide // LANES):
                b = step * (wide // LANES) + i
                s = scores_ref[here, pl.ds(pl.multiple_of(b * LANES, LANES), LANES)]
                t = teach_ref[pl.ds(pl.multiple_of(b * rows + g * group, group), group), :]
                gap = s - peak
                coef = jnp.where(t < 0.0, gap - t + named_add, tail_add)
                grad_ref[here, i * LANES : (i + 1) * LANES] = (jnp.exp(gap) * scale * coef).astype(BF16)
        cols = pl.ds(pl.multiple_of(step * wide, wide), wide)
        g_block = grad_ref[...]
        acc_ref[...] += contract(g_block, up_ref[:, cols], ((1,), (1,)))
        b_part[:, cols] = jnp.dot(low_rank_t, g_block, preferred_element_type=F32).astype(BF16)

    back_buf[sec] = acc_ref[...].astype(BF16)
    back_swap = SectionExchange(back_buf, sec_send.at[2], sec_recv.at[2], n_sec)
    back_swap.start()
    b_sum = DataReduce(b_part, b_pair, b_slots, b_total, b_sems, n_dp)
    a_sum = DataReduce(a_part, a_pair, a_slots, a_total, a_sems, n_dp)
    b_sum.start_pair()

    loss_pair.wait()
    loss_part[2] = loss_part[0] + loss_part[1]
    loss_copies = []
    for j in range(1, n2):
        c = remote(
            loss_part.at[2],
            loss_slots.at[j - 1],
            loss_sems.at[0, j],
            loss_sems.at[1, j],
            "dp",
            lax.rem(chip + j, n2) * 2 + core,
        )
        c.start()
        loss_copies.append(c)

    b_sum.start_scatter()
    back_swap.wait()
    back_sum = back_buf[0].astype(F32)
    for s in range(1, n_sec):
        back_sum = back_sum + back_buf[s].astype(F32)
    back_t = back_sum.T.astype(BF16)
    a_part[:, 0:features] = jnp.dot(back_t, hidden_ref[...], preferred_element_type=F32).astype(BF16)
    a_sum.start_pair()
    a_sum.start_scatter()
    b_sum.start_gather()
    a_sum.start_gather()

    loss_all = loss_part[2]
    for j in range(1, n2):
        loss_copies[j - 1].wait()
        loss_all = loss_all + loss_slots[j - 1]
    count_all = loss_all[0:1, 1:2]
    loss_ref[...] = loss_all / count_all
    factor = SCALE_LOSS / count_all

    b_sum.forward()
    a_sum.forward()
    grad_b_ref[...] = b_total[:, 0:width].astype(F32) * factor
    grad_a_ref[...] = a_total[:, 0:features].astype(F32) * factor


def padded(columns, n):
    unit = LANES * n
    return (columns + unit - 1) // unit * unit


def body(
    n_sec,
    n_dp,
    student_head_logits,
    hidden,
    adapter_down,
    adapter_up,
    teacher_top_index,
    teacher_top_values,
    teacher_other_logit,
    lengths,
):
    seq_total, seq_len, width = student_head_logits.shape
    rows = seq_total * seq_len
    features = hidden.shape[2]
    topk = teacher_top_index.shape[2]
    rank = adapter_up.shape[0]
    n2 = n_dp // 2
    b_width, a_width = padded(width, n_dp), padded(features, n_dp)
    vmem = pl.BlockSpec(memory_space=pltpu.VMEM)

    def reduce_scratch(columns):
        return [
            pltpu.VMEM((rank, columns), BF16),
            pltpu.VMEM((rank, columns // 2), BF16),
            pltpu.VMEM((n2 - 1, rank, columns // n_dp), BF16),
            pltpu.VMEM((rank, columns), BF16),
        ]

    loss, grad_a, grad_b = pl.pallas_call(
        functools.partial(kernel, n_sec, n_dp, seq_len),
        out_shape=(
            jax.ShapeDtypeStruct((8, LANES), F32),
            jax.ShapeDtypeStruct((rank, features), F32),
            jax.ShapeDtypeStruct((rank, width), F32),
        ),
        in_specs=[pl.BlockSpec(memory_space=pltpu.SMEM)] + [vmem] * 7,
        out_specs=(vmem, vmem, vmem),
        scratch_shapes=[
            pltpu.VMEM((rows, width), F32),
            pltpu.VMEM((rows * (width // LANES), LANES), F32),
            pltpu.VMEM((rows, 512), BF16),
            pltpu.VMEM((rows, LANES), F32),
            pltpu.VMEM((rows, LANES), F32),
            pltpu.VMEM((rows, LANES), F32),
            pltpu.VMEM((n_sec, rows, rank), BF16),
            pltpu.VMEM((n_sec, rows, LANES), F32),
            pltpu.VMEM((n_sec, rows, rank), BF16),
            pltpu.VMEM((rows, rank), F32),
            pltpu.VMEM((4, rows, LANES), F32),
            *reduce_scratch(b_width),
            *reduce_scratch(a_width),
            pltpu.VMEM((3, 8, LANES), F32),
            pltpu.VMEM((n2 - 1, 8, LANES), F32),
            pltpu.SemaphoreType.DMA((3, n_sec - 1)),
            pltpu.SemaphoreType.DMA((3, n_sec - 1)),
            pltpu.SemaphoreType.DMA((8, n2)),
            pltpu.SemaphoreType.DMA((8, n2)),
            pltpu.SemaphoreType.DMA((2, n2)),
        ],
        compiler_params=pltpu.CompilerParams(
            collective_id=0, has_side_effects=True, vmem_limit_bytes=60 * 1024 * 1024
        ),
    )(
        lengths,
        student_head_logits.reshape(rows, width),
        hidden.reshape(rows, features),
        adapter_down,
        adapter_up,
        teacher_top_index.reshape(rows, topk),
        teacher_top_values.reshape(rows, topk),
        teacher_other_logit,
    )
    return (loss[0, 0], grad_a.T, grad_b)


def solution(mesh):
    return jax.shard_map(
        functools.partial(body, mesh.shape["section"], mesh.shape["dp"]),
        mesh=mesh,
        in_specs=(
            P("dp", None, "section"),
            P("dp", None, "section"),
            P("section", None),
            P(None, "section"),
            P("dp", None, None),
            P("dp", None, None),
            P("dp", None),
            P("dp"),
        ),
        out_specs=(P(), P("section", None), P(None, "section")),
        check_vma=False,
    )
```

time: 367 us -> 86.3 us (0.24); the launches traced: 363 us -> 86 us
  local copies, waits for them, and re-layouts: 179 us -> 10.7 us
  Pallas kernels: 0 us -> 74.6 us
  waiting for transfers between devices: 65.9 us -> 0 us
  blocking collectives: 59.1 us -> 0 us
  other arithmetic: 29.5 us -> 0 us
  between operations: 17.7 us -> 0.64 us
  matrix products: 11.4 us -> 0 us
    gather x5 -> x0, local copies, waits for them, and re-layouts: 111 us -> none  [body(): jnp.take_along_axis(logit_scores, jnp.clip(local_ids, 0, slice_width - 1)...]
    pallas_call x0 -> x1, Pallas kernels: none -> 74.6 us  [body(): pl.pallas_call(functools.partial(kernel, n_sec, n_dp, seq_len), out_shape...]
    psum x1 -> x0, waiting for transfers between devices: 65.9 us -> none  [body(): lax.psum((grad_b, grad_a, loss_sum, token_count), 'dp')]
    psum x4 -> x0, blocking collectives: 54.2 us -> none  [the longest x1 36.1 us: body(): lax.psum((grad_b, grad_a, loss_sum, token_count), 'dp')]
    unnamed x18 -> x5, local copies, waits for them, and re-layouts: 47.6 us -> 9.54 us
    dot_general x5 -> x0, matrix products: 11.4 us -> none  [the longest x1 6.69 us: body(): jnp.dot(reduced_features, adapter_up, preferred_element_type=jnp.float32)]
    sub x5 -> x0, local copies, waits for them, and re-layouts: 9.75 us -> none  [the longest x1 9.46 us: body(): 1.0 - support]
    scatter x1 -> x0, local copies, waits for them, and re-layouts: 9.39 us -> none  [body(): log_gap = jnp.broadcast_to(log_ratio_tail[:, None], (row_count, slice_wid...]
  transfers between devices with their start and end apart: 1 -> 0, of which waited for: 1 -> 0; matrix products, arithmetic and copies ran while one was open for 0% -> 0% of each run, Pallas kernels for 0% -> 0%
where the time goes in v1:
time: 86.3 us; the launch traced here: 86 us
  Pallas kernels  74.6 us (86%)
  local copies, waits for them, and re-layouts  10.7 us (12%)
    pallas_call x1, Pallas kernels, body(): pl.pallas_call(functools.partial(kernel, n_sec, n_dp, seq_len), out_shape...  74.6 us
    unnamed x5, local copies, waits for them, and re-layouts  9.54 us

profile of v1, /device:TPU:0, one launch (start us, length us, event | category | flops | bytes accessed | tf_op | source)
XLA Modules:
  0.0 86.0 jit_solution(7065754893234130150)
XLA Ops:
  0.6 1.5 %copy.11 = s32[2,64,32]{2,1,0:T(8,128)} copy(s32[2,64,32]{1,2,0:T(8,128)} %param.12) | data formatting | bytes 32768 | tf_op args[4]
  2.1 1.5 %copy.12 = f32[2,64,32]{2,1,0:T(8,128)} copy(f32[2,64,32]{1,2,0:T(8,128)} %param.13) | data formatting | bytes 32768 | tf_op args[5]
  3.6 1.9 %copy.13.down_ref = bf16[2048,32]{1,0:T(8,128)(2,1)} copy(bf16[2048,32]{0,1:T(8,128)(2,1)} %param.10) | data formatting | bytes 262144 | tf_op args[2]
  5.5 74.6 %shard_map.103 = (f32[8,128]{1,0:T(8,128)}, f32[32,2048]{1,0:T(8,128)}, f32[32,16384]{1,0:T(8,128)}) custom-call(s32[2]{0:T(128)} %lengths_ref.1, bf16[128,16384]{1,0:T(8,128)(2,1)} %bitcast.6, bf16[128,2048]{1,0:T(8,128)(2,1)} %bitcast.7, bf16[2048,32]{1,0:T(8,128)(2,1)} %copy.13.down_ref, bf16[32,16384]{1,0:T(8,128)(2,1)} %up_ref.1, s32[128,32]{1,0:T(8,128)} %bitcast.8, ...), custom_call_target="tpu_custom_call" | custom-call | tf_op jit(solution)/shard_map/pallas_call | solution.py:469
  80.1 1.2 %slice.3 = f32[1,1]{1,0:T(1,128)} slice(f32[8,128]{1,0:T(8,128)} %get-tuple-element.6), slice={[0:1], [0:1]} | slice | bytes 8 | tf_op jit(solution)/shard_map/slice | solution.py:513
  81.3 1.7 %copy.16 = f32[2048,32]{0,1:T(8,128)} copy(f32[2048,32]{0,1:T(8,128)} %bitcast.10) | data formatting | bytes 524288
  82.9 3.0 %copy.17 = f32[32,16384]{1,0:T(8,128)} copy(f32[32,16384]{1,0:T(8,128)} %get-tuple-element.14) | data formatting | bytes 4194304

commit v2 on v1

--- a/solution.py
+++ b/solution.py
@@ -9,6 +9,9 @@
 
 SCALE_LOSS = 16384.0
 LANES = 128
+SPAN = 1024
+UNROLL = 16
+SCALE_STEPS = 2
 F32 = jnp.float32
 BF16 = jnp.bfloat16
 MESH = pl.DeviceIdType.MESH
@@ -65,46 +68,50 @@
     def order(self):
         return list(range(1, self.n2)) + [0]
 
+    def pair_copy(self, j):
+        piece = lax.rem(self.chip + j, self.n2)
+        return remote(
+            self.part.at[:, self.cols(1 - self.core, piece)],
+            self.pair.at[:, self.cols(0, piece)],
+            self.sems.at[0, j],
+            self.sems.at[1, j],
+            "dp",
+            self.mate,
+        )
+
     def start_pair(self):
-        self.pair_copies = {}
         for j in self.order():
-            piece = lax.rem(self.chip + j, self.n2)
-            c = remote(
-                self.part.at[:, self.cols(1 - self.core, piece)],
-                self.pair.at[:, self.cols(0, piece)],
-                self.sems.at[0, j],
-                self.sems.at[1, j],
-                "dp",
-                self.mate,
-            )
-            c.start()
-            self.pair_copies[j] = c
+            self.pair_copy(j).start()
+
+    def merge_piece(self, j):
+        piece = lax.rem(self.chip + j, self.n2)
+        self.pair_copy(j).wait()
+        mine = self.cols(self.core, piece)
+        both = self.part[:, mine].astype(F32) + self.pair[:, self.cols(0, piece)].astype(F32)
+        self.part[:, mine] = both.astype(BF16)
+
+    def scatter_copy(self, j):
+        piece = lax.rem(self.chip + j, self.n2)
+        return remote(
+            self.part.at[:, self.cols(self.core, piece)],
+            self.slots.at[j - 1],
+            self.sems.at[2, j],
+            self.sems.at[3, j],
+            "dp",
+            self.peer(j),
+        )
 
     def start_scatter(self):
-        self.scatter_copies = {}
         for j in self.order():
-            piece = lax.rem(self.chip + j, self.n2)
-            self.pair_copies[j].wait()
-            mine = self.cols(self.core, piece)
-            both = self.part[:, mine].astype(F32) + self.pair[:, self.cols(0, piece)].astype(F32)
-            self.part[:, mine] = both.astype(BF16)
+            self.merge_piece(j)
             if j:
-                c = remote(
-                    self.part.at[:, mine],
-                    self.slots.at[j - 1],
-                    self.sems.at[2, j],
-                    self.sems.at[3, j],
-                    "dp",
-                    self.peer(j),
-                )
-                c.start()
-                self.scatter_copies[j] = c
+                self.scatter_copy(j).start()
 
     def start_gather(self):
         mine = self.cols(self.core, self.chip)
         acc = self.part[:, mine].astype(F32)
         for j in range(1, self.n2):
-            self.scatter_copies[j].wait()
+            self.scatter_copy(j).wait()
             acc = acc + self.slots[j - 1].astype(F32)
         self.total[:, mine] = acc.astype(BF16)
         self.gather_copies = {}
@@ -150,16 +157,19 @@
     n_dp,
     seq_len,
     lengths_ref,
-    logits_ref,
+    logits_hbm,
     hidden_ref,
     down_ref,
-    up_ref,
+    up_hbm,
     ids_ref,
     values_ref,
     other_ref,
     loss_ref,
-    grad_a_ref,
-    grad_b_ref,
+    a_total,
+    b_total,
+    logits_ref,
+    up_ref,
+    load_sems,
     scores_ref,
     teach_ref,
     grad_ref,
@@ -174,11 +184,9 @@
     b_part,
     b_pair,
     b_slots,
-    b_total,
     a_part,
     a_pair,
     a_slots,
-    a_total,
     loss_part,
     loss_slots,
     sec_send,
@@ -199,6 +207,10 @@
     chip = me // 2
     mate = me + 1 - 2 * core
 
+    logits_load = pltpu.make_async_copy(logits_hbm, logits_ref, load_sems.at[0])
+    up_load = pltpu.make_async_copy(up_hbm, up_ref, load_sems.at[1])
+    up_load.start()
+    logits_load.start()
     barrier = pltpu.get_barrier_semaphore()
     for j in range(1, n_sec):
         pl.semaphore_signal(barrier, inc=1, device_id={"section": lax.rem(sec + j, n_sec)}, device_id_type=MESH)
@@ -208,14 +220,14 @@
             barrier, inc=1, device_id={"dp": lax.rem(chip + j, n2) * 2 + core}, device_id_type=MESH
         )
 
-    low_part = jnp.dot(hidden_ref[...], down_ref[...], preferred_element_type=F32)
+    low_part = contract(hidden_ref[...], down_ref[...], ((1,), (1,)))
     low_buf[sec] = low_part.astype(BF16)
     pl.semaphore_wait(barrier, n_sec - 1 + 1 + n2 - 1)
     low_swap = SectionExchange(low_buf, sec_send.at[0], sec_recv.at[0], n_sec)
     low_swap.start()
 
-    values = values_ref[...]
     seq_total = rows // seq_len
+    values = jnp.concatenate([values_ref[s].T for s in range(seq_total)], axis=0)
     eye = lax.broadcasted_iota(jnp.int32, (seq_len, seq_len), 0) == lax.broadcasted_iota(
         jnp.int32, (seq_len, seq_len), 1
     )
@@ -236,7 +248,7 @@
     first = shifted.astype(BF16).astype(F32)
     second = (shifted - first).astype(BF16).astype(F32)
     third = shifted - first - second
-    ids = ids_ref[...]
+    ids = jnp.concatenate([ids_ref[s].T for s in range(seq_total)], axis=0)
     high = ((ids >> 7) - sec * blocks).astype(F32)
     low = (ids & (LANES - 1)).astype(F32)
     hi_ref[...] = jnp.full((rows, LANES), -1.0, F32)
@@ -257,7 +269,7 @@
             left.astype(BF16), right.astype(BF16), ((1,), (1,))
         )
 
-    unroll = 4
+    unroll = UNROLL
 
     @pl.loop(0, rows // unroll)
     def _(step):
@@ -265,13 +277,15 @@
             place_row(step * unroll + u)
 
     low_swap.wait()
+    up_load.wait()
+    logits_load.wait()
     low_sum = low_buf[0].astype(F32)
     for s in range(1, n_sec):
         low_sum = low_sum + low_buf[s].astype(F32)
     low_rank = low_sum.astype(BF16)
     low_rank_t = low_sum.T.astype(BF16)
 
-    span = 256
+    span = SPAN
 
     def score_step(step, top):
         cols = pl.ds(pl.multiple_of(step * span, span), span)
@@ -364,10 +378,11 @@
         b_part[:, width:] = jnp.zeros((rank, b_part.shape[1] - width), BF16)
     if a_part.shape[1] > features:
         a_part[:, features:] = jnp.zeros((rank, a_part.shape[1] - features), BF16)
-    wide = 512
-
-    @pl.loop(0, width // wide)
-    def _(step):
+    b_sum = DataReduce(b_part, b_pair, b_slots, b_total, b_sems, n_dp)
+    a_sum = DataReduce(a_part, a_pair, a_slots, a_total, a_sems, n_dp)
+    wide = grad_ref.shape[1]
+
+    def grad_step(step):
         for g in range(rows // group):
             here = pl.ds(g * group, group)
             peak, scale = row_ref[0, here, :], row_ref[1, here, :]
@@ -384,12 +399,33 @@
         acc_ref[...] += contract(g_block, up_ref[:, cols], ((1,), (1,)))
         b_part[:, cols] = jnp.dot(low_rank_t, g_block, preferred_element_type=F32).astype(BF16)
 
+    def grad_piece(half, piece):
+        first_step = (half * b_sum.half + piece * b_sum.width) // wide
+
+        @pl.when(first_step * wide < width)
+        def _():
+            for i in range(b_sum.width // wide):
+                grad_step(first_step + i)
+
+    @pl.loop(0, n2)
+    def _(i):
+        j = lax.rem(i + 1, n2)
+        grad_piece(1 - core, lax.rem(chip + j, n2))
+        b_sum.pair_copy(j).start()
+
+    @pl.loop(0, n2)
+    def _(i):
+        j = lax.rem(i + 1, n2)
+        grad_piece(core, lax.rem(chip + j, n2))
+        b_sum.merge_piece(j)
+
+        @pl.when(i < n2 - 1)
+        def _():
+            b_sum.scatter_copy(j).start()
+
     back_buf[sec] = acc_ref[...].astype(BF16)
     back_swap = SectionExchange(back_buf, sec_send.at[2], sec_recv.at[2], n_sec)
     back_swap.start()
-    b_sum = DataReduce(b_part, b_pair, b_slots, b_total, b_sems, n_dp)
-    a_sum = DataReduce(a_part, a_pair, a_slots, a_total, a_sems, n_dp)
-    b_sum.start_pair()
 
     loss_pair.wait()
     loss_part[2] = loss_part[0] + loss_part[1]
@@ -406,7 +442,6 @@
         c.start()
         loss_copies.append(c)
 
-    b_sum.start_scatter()
     back_swap.wait()
     back_sum = back_buf[0].astype(F32)
     for s in range(1, n_sec):
@@ -422,14 +457,18 @@
     for j in range(1, n2):
         loss_copies[j - 1].wait()
         loss_all = loss_all + loss_slots[j - 1]
-    count_all = loss_all[0:1, 1:2]
-    loss_ref[...] = loss_all / count_all
-    factor = SCALE_LOSS / count_all
+    loss_ref[...] = loss_all
 
     b_sum.forward()
     a_sum.forward()
-    grad_b_ref[...] = b_total[:, 0:width].astype(F32) * factor
-    grad_a_ref[...] = a_total[:, 0:features].astype(F32) * factor
+
+
+def scale_kernel(sums_ref, a_ref, b_ref, loss_ref, grad_a_ref, grad_b_ref):
+    count = sums_ref[0:1, 1:2]
+    factor = SCALE_LOSS / count
+    loss_ref[...] = sums_ref[0:1, 0:1] / count
+    grad_a_ref[...] = a_ref[...].astype(F32) * factor
+    grad_b_ref[...] = b_ref[...].astype(F32) * factor
 
 
 def padded(columns, n):
@@ -457,28 +496,31 @@
     n2 = n_dp // 2
     b_width, a_width = padded(width, n_dp), padded(features, n_dp)
     vmem = pl.BlockSpec(memory_space=pltpu.VMEM)
+    hbm = pl.BlockSpec(memory_space=pltpu.HBM)
 
     def reduce_scratch(columns):
         return [
             pltpu.VMEM((rank, columns), BF16),
             pltpu.VMEM((rank, columns // 2), BF16),
             pltpu.VMEM((n2 - 1, rank, columns // n_dp), BF16),
-            pltpu.VMEM((rank, columns), BF16),
         ]
 
-    loss, grad_a, grad_b = pl.pallas_call(
+    sums, a_total, b_total = pl.pallas_call(
         functools.partial(kernel, n_sec, n_dp, seq_len),
         out_shape=(
             jax.ShapeDtypeStruct((8, LANES), F32),
-            jax.ShapeDtypeStruct((rank, features), F32),
-            jax.ShapeDtypeStruct((rank, width), F32),
+            jax.ShapeDtypeStruct((rank, a_width), BF16),
+            jax.ShapeDtypeStruct((rank, b_width), BF16),
         ),
-        in_specs=[pl.BlockSpec(memory_space=pltpu.SMEM)] + [vmem] * 7,
+        in_specs=[pl.BlockSpec(memory_space=pltpu.SMEM), hbm, vmem, vmem, hbm] + [vmem] * 3,
         out_specs=(vmem, vmem, vmem),
         scratch_shapes=[
+            pltpu.VMEM((rows, width), BF16),
+            pltpu.VMEM((rank, width), BF16),
+            pltpu.SemaphoreType.DMA((2,)),
             pltpu.VMEM((rows, width), F32),
             pltpu.VMEM((rows * (width // LANES), LANES), F32),
-            pltpu.VMEM((rows, 512), BF16),
+            pltpu.VMEM((rows, min(1024, b_width // n_dp)), BF16),
             pltpu.VMEM((rows, LANES), F32),
             pltpu.VMEM((rows, LANES), F32),
             pltpu.VMEM((rows, LANES), F32),
@@ -504,12 +546,31 @@
         lengths,
         student_head_logits.reshape(rows, width),
         hidden.reshape(rows, features),
-        adapter_down,
+        adapter_down.T,
         adapter_up,
-        teacher_top_index.reshape(rows, topk),
-        teacher_top_values.reshape(rows, topk),
+        jnp.swapaxes(teacher_top_index, 1, 2),
+        jnp.swapaxes(teacher_top_values, 1, 2),
         teacher_other_logit,
     )
+    loss, grad_a, grad_b = pl.pallas_call(
+        scale_kernel,
+        out_shape=(
+            jax.ShapeDtypeStruct((1, 1), F32),
+            jax.ShapeDtypeStruct((rank, features), F32),
+            jax.ShapeDtypeStruct((rank, width), F32),
+        ),
+        grid=(SCALE_STEPS,),
+        in_specs=[
+            pl.BlockSpec((8, LANES), lambda i: (0, 0)),
+            pl.BlockSpec((rank, features // SCALE_STEPS), lambda i: (0, i)),
+            pl.BlockSpec((rank, width // SCALE_STEPS), lambda i: (0, i)),
+        ],
+        out_specs=(
+            pl.BlockSpec((1, 1), lambda i: (0, 0)),
+            pl.BlockSpec((rank, features // SCALE_STEPS), lambda i: (0, i)),
+            pl.BlockSpec((rank, width // SCALE_STEPS), lambda i: (0, i)),
+        ),
+    )(sums, a_total, b_total)
     return (loss[0, 0], grad_a.T, grad_b)
 
 

time: 86.3 us -> 63.7 us (0.74)
  Pallas kernels: 74.6 us -> 62.9 us
  local copies, waits for them, and re-layouts: 10.7 us -> 0 us
    pallas_call x1, Pallas kernels: 74.6 us -> 60.2 us  [body(): pl.pallas_call(functools.partial(kernel, n_sec, n_dp, seq_len), out_shape...]
    unnamed x5 -> x0, local copies, waits for them, and re-layouts: 9.54 us -> none
    pallas_call x0 -> x1, Pallas kernels: none -> 2.65 us  [body(): pl.pallas_call(scale_kernel, out_shape=(jax.ShapeDtypeStruct((1, 1), F32)...]
    slice x1 -> x0, local copies, waits for them, and re-layouts: 1.19 us -> none  [body(): return (loss[0, 0], grad_a.T, grad_b)]
where the time goes in v2:
time: 63.7 us; the launch traced here: 63.5 us
  Pallas kernels  62.9 us (99%)
  between operations  0.64 us (1%)
    pallas_call x1, Pallas kernels, body(): pl.pallas_call(functools.partial(kernel, n_sec, n_dp, seq_len), out_shape...  60.2 us
    pallas_call x1, Pallas kernels, body(): pl.pallas_call(scale_kernel, out_shape=(jax.ShapeDtypeStruct((1, 1), F32)...  2.65 us

profile of v2, /device:TPU:0, one launch (start us, length us, event | category | flops | bytes accessed | tf_op | source)
XLA Modules:
  0.0 63.5 jit_solution(2197388262714133436)
XLA Ops:
  0.6 60.2 %shard_map.103 = (f32[8,128]{1,0:T(8,128)}, bf16[32,2048]{1,0:T(8,128)(2,1)}, bf16[32,16384]{1,0:T(8,128)(2,1)}) custom-call(s32[2]{0:T(128)} %lengths_ref.1, bf16[128,16384]{1,0:T(8,128)(2,1)} %bitcast.7, bf16[128,2048]{1,0:T(8,128)(2,1)} %bitcast.8, bf16[32,2048]{1,0:T(8,128)(2,1)} %bitcast.9, bf16[32,16384]{1,0:T(8,128)(2,1)} %up_hbm.1, ...), custom_call_target="tpu_custom_call" | custom-call | tf_op jit(solution)/shard_map/pallas_call | solution.py:508
  60.9 2.7 %shard_map.104 = (f32[1,1]{1,0:T(1,128)}, f32[32,2048]{1,0:T(8,128)}, f32[32,16384]{1,0:T(8,128)}) custom-call(f32[8,128]{1,0:T(8,128)} %get-tuple-element.9.sums_ref, bf16[32,2048]{1,0:T(8,128)(2,1)} %get-tuple-element.10.a_ref, bf16[32,16384]{1,0:T(8,128)(2,1)} %get-tuple-element.11.b_ref), custom_call_target="tpu_custom_call" | custom-call | tf_op jit(solution)/shard_map/pallas_call | solution.py:555

commit v3 on v2

--- a/solution.py
+++ b/solution.py
@@ -9,8 +9,8 @@
 
 SCALE_LOSS = 16384.0
 LANES = 128
-SPAN = 1024
-UNROLL = 16
+SPAN = 2048
+UNROLL = 32
 SCALE_STEPS = 2
 F32 = jnp.float32
 BF16 = jnp.bfloat16
@@ -305,7 +305,7 @@
 
     group = 32
     lane = lax.broadcasted_iota(jnp.int32, (group, LANES), 1)
-    chunk = 4
+    chunk = 8
 
     @pl.loop(0, rows // group)
     def _(g):

time: 63.7 us -> 62.1 us (0.975)
  Pallas kernels: 62.9 us -> 61.3 us
    pallas_call x1, Pallas kernels: 60.2 us -> 58.6 us  [body(): pl.pallas_call(functools.partial(kernel, n_sec, n_dp, seq_len), out_shape...]
where the time goes in v3:
time: 62.1 us; the launch traced here: 61.9 us
  Pallas kernels  61.3 us (99%)
  between operations  0.64 us (1%)
    pallas_call x1, Pallas kernels, body(): pl.pallas_call(functools.partial(kernel, n_sec, n_dp, seq_len), out_shape...  58.6 us
    pallas_call x1, Pallas kernels, body(): pl.pallas_call(scale_kernel, out_shape=(jax.ShapeDtypeStruct((1, 1), F32)...  2.65 us

profile of v3, /device:TPU:0, one launch (start us, length us, event | category | flops | bytes accessed | tf_op | source)
XLA Modules:
  0.0 61.9 jit_solution(17813348173683957090)
XLA Ops:
  0.6 58.6 %shard_map.103 = (f32[8,128]{1,0:T(8,128)}, bf16[32,2048]{1,0:T(8,128)(2,1)}, bf16[32,16384]{1,0:T(8,128)(2,1)}) custom-call(s32[2]{0:T(128)} %lengths_ref.1, bf16[128,16384]{1,0:T(8,128)(2,1)} %bitcast.7, bf16[128,2048]{1,0:T(8,128)(2,1)} %bitcast.8, bf16[32,2048]{1,0:T(8,128)(2,1)} %bitcast.9, bf16[32,16384]{1,0:T(8,128)(2,1)} %up_hbm.1, ...), custom_call_target="tpu_custom_call" | custom-call | tf_op jit(solution)/shard_map/pallas_call | solution.py:508
  59.3 2.7 %shard_map.104 = (f32[1,1]{1,0:T(1,128)}, f32[32,2048]{1,0:T(8,128)}, f32[32,16384]{1,0:T(8,128)}) custom-call(f32[8,128]{1,0:T(8,128)} %get-tuple-element.9.sums_ref, bf16[32,2048]{1,0:T(8,128)(2,1)} %get-tuple-element.10.a_ref, bf16[32,16384]{1,0:T(8,128)(2,1)} %get-tuple-element.11.b_ref), custom_call_target="tpu_custom_call" | custom-call | tf_op jit(solution)/shard_map/pallas_call | solution.py:555
